TPU v7x, 32 devices: a whole 2x2x4 slice. The times are simulated.
32 devices in a mesh: pair: 2 (over y), dp: 8 (over z, x), ep: 2 (over core).
Axes of the slice: x: 2, y: 2, z: 4, core: 2. Of those that a mesh axis runs over, the one named last changes fastest.
Arguments:
- activations: bfloat16 [12288, 1024], P(('pair', 'dp'), 'ep'), parts along dimension 1, may hold values from -6 to 6
- cotangents: bfloat16 [12288, 4096], P(('pair', 'dp'), 'ep'), parts along dimension 1, may hold values from -0.875 to 0.875
Outputs:
- averaged_grad: bfloat16 [512, 4096], P('pair', 'ep'), parts along dimension 1
There are 2 independent parts, one for each index of `ep`. A program takes and returns all parts, laid end to end along the dimension named above; each array names one. Nothing has to cross between parts.
All inputs are finite; a program needn't handle non-finite values.
Results may differ from a plain program's by a relative error of at most 0.001.
Values may be sent and summed in bfloat16 or wider, within the bound.
A program may use at most 64 MiB of HBM per device.

v0:
```python
import jax
import jax.numpy as jnp
from jax import lax
from jax.sharding import PartitionSpec as P


def local(activations, cotangents):
    replicas = lax.axis_size("pair") * lax.axis_size("dp")
    partial_grad = lax.dot_general(
        activations, cotangents, (((0,), (0,)), ((), ())), preferred_element_type=jnp.float32
    )
    summed = lax.psum_scatter(partial_grad, ("pair", "dp"), scatter_dimension=0, tiled=True)
    averaged = (summed / replicas).astype(jnp.bfloat16)
    return lax.all_gather(averaged, "dp", axis=0, tiled=True)


def solution(mesh):
    in_specs = (P(("pair", "dp"), "ep"), P(("pair", "dp"), "ep"))
    out_specs = P("pair", "ep")
    return jax.shard_map(local, mesh=mesh, in_specs=in_specs, out_specs=out_specs, check_vma=False)
```

profile of v0, /device:TPU:0, one launch (start us, length us, event | category | flops | bytes accessed | tf_op | source)
XLA Modules:
  0.0 163.2 jit_solution(17401079811682775837)
XLA Ops:
  6.5 0.0 copy-start
  6.5 0.0 reduce-scatter.2.cloned.1.call-start
  6.5 1.9 %copy-done = bf16[768,2048]{1,0:T(8,128)(2,1)S(1)} copy-done((bf16[768,2048]{1,0:T(8,128)(2,1)S(1)}, bf16[768,2048]{1,0:T(8,128)(2,1)}, u32[]{:S(2)}) %copy-start) | copy-done | bytes 3145752
  8.4 4.9 %fusion = f32[512,2048]{1,0:T(8,128)} fusion(bf16[768,512]{1,0:T(8,128)(2,1)} %param.2, bf16[768,2048]{1,0:T(8,128)(2,1)S(1)} %copy-done), kind=kOutput, calls=%fused_computation.1 | convolution fusion | flops 1610612736 | bytes 8126464 | tf_op jit(solution)/shard_map/dot_general | solution.py:9
  13.3 0.0 reduce-scatter.2.cloned.1.call-update
  13.3 0.0 all-gather.2.cloned.1.call-start
  13.4 100.0 %reduce-scatter.2.cloned.1.call-done = f32[32,2048]{1,0:T(8,128)} async-done(((f32[512,2048]{1,0:T(8,128)}), f32[32,2048]{1,0:T(8,128)}) %reduce-scatter.2.cloned.1.call-update) | async-done | bytes 262160 | tf_op jit(solution)/shard_map/reduce_scatter | solution.py:12
  113.4 1.6 multiply_convert_fusion
  115.0 0.0 all-gather.2.cloned.1.call-update
  115.0 39.1 %all-gather.2.cloned.1.call-done = bf16[256,2048]{1,0:T(8,128)(2,1)} async-done(((bf16[32,2048]{1,0:T(8,128)(2,1)}), bf16[256,2048]{1,0:T(8,128)(2,1)}) %all-gather.2.cloned.1.call-update) | async-done | bytes 1048592 | tf_op jit(solution)/shard_map/all_gather | solution.py:14
  154.1 2.3 %copy.4 = bf16[256,2048]{1,0:T(8,128)(2,1)} copy(bf16[256,2048]{1,0:T(8,128)(2,1)} %all-gather.2.cloned.1.call-done) | data formatting | bytes 2097152
Async XLA Ops:
  6.5 1.9 %copy-start = (bf16[768,2048]{1,0:T(8,128)(2,1)S(1)}, bf16[768,2048]{1,0:T(8,128)(2,1)}, u32[]{:S(2)}) copy-start(bf16[768,2048]{1,0:T(8,128)(2,1)} %param.3) | copy-start | bytes 9437188
  6.5 106.8 %reduce-scatter.2.cloned.1.call-start = ((), (), s32[]{:S(2)}) async-start(), calls=%async_computation.1 | async-start | bytes 4456448 | tf_op jit(solution)/shard_map/reduce_scatter | solution.py:12
  13.3 140.7 %all-gather.2.cloned.1.call-start = ((), (), s32[]{:S(2)}) async-start(), calls=%async_computation.2 | async-start | bytes 1179648 | tf_op jit(solution)/shard_map/all_gather | solution.py:14
Sparse Core Ops, SparseCore 0:
  13.5 99.8 reduce-scatter.1
  115.5 38.5 all-gather.1
where the time goes:
time: 163 us
  waiting for transfers between devices  139 us (85%)
  between operations  13.4 us (8%)
  matrix products  4.9 us (3%)
  local copies, waits for them, and re-layouts  4.19 us (3%)
    reduce_scatter x1, waiting for transfers between devices, local(): lax.psum_scatter(partial_grad, ('pair', 'dp'), scatter_dimension=0, tiled...  100 us
    all_gather x1, waiting for transfers between devices, local(): return lax.all_gather(averaged, 'dp', axis=0, tiled=True)  39.1 us
    dot_general x1, matrix products, local(): lax.dot_general(activations, cotangents, (((0,), (0,)), ((), ())), prefer...  4.9 us
    unnamed x3, local copies, waits for them, and re-layouts  4.19 us
  transfers between devices with their start and end apart: 2, of which 2 were waited for; matrix products, arithmetic and copies ran while one was open for 0% of the time, Pallas kernels for 0%

commit v1 on v0

v1 whole, which is shorter than its diff:
```python
import functools

import jax
import jax.numpy as jnp
from jax import lax
from jax.experimental import pallas as pl
from jax.experimental.pallas import tpu as pltpu
from jax.sharding import PartitionSpec as P

LANES = 128
SPLIT = 2
AHEAD = 4
CROSS = 4


def kernel(np_, nx, nz, nc, ns, act_ref, cot_ref, out_ref, act_t, part, f1, f2, zr,
           s1, r1, s2, r2, sz, rz, sg, rg, sx, rx):
    p = lax.axis_index("pair")
    dp = lax.axis_index("dp")
    z, x = dp // nx, dp % nx
    rs = part.shape[-2]
    chunks = nc * ns
    rows_p = nz * ns * rs
    cols_x = nc * LANES

    def other(i, q, n):
        return lax.rem(i + q, n)

    def to_pair(q):
        return {"pair": other(p, q, np_)}

    def to_x(q):
        return {"dp": z * nx + other(x, q, nx)}

    def to_z(q):
        return {"dp": other(z, q, nz) * nx + x}

    def crossed(k):
        return lax.rem(k // ns, CROSS) == CROSS - 1

    def remote(src, dst, ssem, rsem, peer):
        return pltpu.make_async_remote_copy(
            src_ref=src, dst_ref=dst, send_sem=ssem, recv_sem=rsem,
            device_id=peer, device_id_type=pl.DeviceIdType.MESH)

    def first_a(k, q):
        return remote(part.at[k, other(p, q, np_)], f1.at[k, pl.ds(p * nx, nx)],
                      s1.at[k, q], r1.at[k, p], to_pair(q))

    def first_b(k, q):
        return remote(part.at[k, :, other(x, q, nx)], f1.at[k, pl.ds(x * np_, np_)],
                      s1.at[k, q], r1.at[k, x], to_x(q))

    def second_a(k, q):
        return remote(part.at[k, p, other(x, q, nx)], f2.at[k, x], s2.at[k, q], r2.at[k, x], to_x(q))

    def second_b(k, q):
        return remote(part.at[k, other(p, q, np_), x], f2.at[k, p], s2.at[k, q], r2.at[k, p], to_pair(q))

    def along_z(k, q):
        return remote(part.at[k, p, x, other(z, q, nz)], zr.at[k, z], sz.at[k, q], rz.at[k, z], to_z(q))

    def piece(k, zi, xi):
        c, s = k // ns, lax.rem(k, ns)
        row = pl.multiple_of((zi * ns + s) * rs, rs)
        col = pl.multiple_of(xi * cols_x + c * LANES, LANES)
        return out_ref.at[pl.ds(row, rs), pl.ds(col, LANES)]

    def gather_z(k, q):
        here = piece(k, z, x)
        return remote(here, here, sg.at[k, q], rg.at[k, z], to_z(q))

    def gather_x(k, zo, q):
        zi = other(z, zo, nz)
        here = piece(k, zi, x)
        return remote(here, here, sx.at[k, zi, q], rx.at[k, zi, x], to_x(q))

    def arrived(dst, ssem, rsem):
        remote(dst, dst, ssem, rsem, to_pair(1)).wait_recv()

    def start_first(k):
        @pl.when(crossed(k))
        def _():
            for q in range(1, nx):
                first_b(k, q).start()

        @pl.when(jnp.logical_not(crossed(k)))
        def _():
            for q in range(1, np_):
                first_a(k, q).start()

    def stage2(k):
        @pl.when(jnp.logical_not(crossed(k)))
        def _():
            for q in range(1, np_):
                o = other(p, q, np_)
                arrived(f1.at[k, pl.ds(o * nx, nx)], s1.at[k, q], r1.at[k, o])
                for i in range(nx):
                    part[k, p, i] += f1[k, o * nx + i]
            for q in range(1, nx):
                second_a(k, q).start()

        @pl.when(crossed(k))
        def _():
            for q in range(1, nx):
                o = other(x, q, nx)
                arrived(f1.at[k, pl.ds(o * np_, np_)], s1.at[k, q], r1.at[k, o])
                for i in range(np_):
                    part[k, i, x] += f1[k, o * np_ + i]
            for q in range(1, np_):
                second_b(k, q).start()

    def stage3(k):
        @pl.when(jnp.logical_not(crossed(k)))
        def _():
            for q in range(1, nx):
                o = other(x, q, nx)
                arrived(f2.at[k, o], s2.at[k, q], r2.at[k, o])
                part[k, p, x] += f2[k, o]

        @pl.when(crossed(k))
        def _():
            for q in range(1, np_):
                o = other(p, q, np_)
                arrived(f2.at[k, o], s2.at[k, q], r2.at[k, o])
                part[k, p, x] += f2[k, o]

        for q in range(1, nz):
            along_z(k, q).start()

    def stage4(k):
        total = part[k, p, x, z]
        for q in range(1, nz):
            o = other(z, q, nz)
            arrived(zr.at[k, o], sz.at[k, q], rz.at[k, o])
            total = total + zr[k, o]
        replicas = np_ * nx * nz
        piece(k, z, x)[...] = (total / replicas).astype(out_ref.dtype)
        for q in range(1, nz):
            gather_z(k, q).start()
        for q in range(1, nx):
            gather_x(k, 0, q).start()

    def stage5(k):
        for zo in range(1, nz):
            o = other(z, zo, nz)
            arrived(piece(k, o, x), sg.at[k, zo], rg.at[k, o])
            for q in range(1, nx):
                gather_x(k, zo, q).start()

    def stage6(k):
        for zi in range(nz):
            for q in range(1, nx):
                o = other(x, q, nx)
                arrived(piece(k, zi, o), sx.at[k, zi, q], rx.at[k, zi, o])

    def finish(k):
        @pl.when(jnp.logical_not(crossed(k)))
        def _():
            for q in range(1, np_):
                first_a(k, q).wait_send()
            for q in range(1, nx):
                second_a(k, q).wait_send()

        @pl.when(crossed(k))
        def _():
            for q in range(1, nx):
                first_b(k, q).wait_send()
            for q in range(1, np_):
                second_b(k, q).wait_send()

        for q in range(1, nz):
            along_z(k, q).wait_send()
            gather_z(k, q).wait_send()
        for zo in range(nz):
            for q in range(1, nx):
                gather_x(k, zo, q).wait_send()

    barrier = pltpu.get_barrier_semaphore()
    peers = [to_pair(q) for q in range(1, np_)] + [to_x(q) for q in range(1, nx)] + [to_z(q) for q in range(1, nz)]
    for peer in peers:
        pl.semaphore_signal(barrier, inc=1, device_id=peer, device_id_type=pl.DeviceIdType.MESH)

    act_t[...] = act_ref[...].T

    def compute(c):
        for xi in range(nx):
            col = pl.multiple_of(xi * cols_x + c * LANES, LANES)
            grad = jnp.dot(act_t[...], cot_ref[:, pl.ds(col, LANES)], preferred_element_type=jnp.float32)
            for pi in range(np_):
                for zi in range(nz):
                    for s in range(ns):
                        row = pi * rows_p + (zi * ns + s) * rs
                        part[c * ns + s, pi, xi, zi] = grad[row:row + rs]

    compute(0)
    pl.semaphore_wait(barrier, len(peers))
    ahead = min(AHEAD, chunks)

    def send_ready(c):
        for s in range(ns):
            k = c * ns + s
            pl.when(k < ahead)(functools.partial(start_first, k))

    send_ready(0)

    @pl.loop(1, nc)
    def _(c):
        compute(c)
        send_ready(c)

    @pl.loop(0, chunks + 3)
    def _(t):
        pl.when(t + ahead < chunks)(lambda: start_first(t + ahead))
        pl.when(t < chunks)(lambda: stage2(t))
        pl.when((t >= 1) & (t - 1 < chunks))(lambda: stage3(t - 1))
        pl.when((t >= 2) & (t - 2 < chunks))(lambda: stage4(t - 2))
        pl.when(t >= 3)(lambda: stage5(t - 3))

    @pl.loop(0, chunks)
    def _(k):
        stage6(k)
        finish(k)


def solution(mesh):
    np_, ndp = mesh.shape["pair"], mesh.shape["dp"]
    nx = 1
    while (2 * nx) ** 2 <= ndp and ndp % (2 * nx) == 0:
        nx *= 2
    nz = ndp // nx

    def local(activations, cotangents):
        rows, cols = activations.shape[1], cotangents.shape[1]
        nc = cols // nx // LANES
        ns = SPLIT
        rs = rows // np_ // nz // ns
        chunks = nc * ns
        wide = max(np_, nx)
        f32 = jnp.float32
        dma = pltpu.SemaphoreType.DMA
        return pl.pallas_call(
            functools.partial(kernel, np_, nx, nz, nc, ns),
            out_shape=jax.ShapeDtypeStruct((rows // np_, cols), jnp.bfloat16),
            in_specs=[pl.BlockSpec(memory_space=pltpu.VMEM)] * 2,
            out_specs=pl.BlockSpec(memory_space=pltpu.VMEM),
            scratch_shapes=[
                pltpu.VMEM((rows, activations.shape[0]), activations.dtype),
                pltpu.VMEM((chunks, np_, nx, nz, rs, LANES), f32),
                pltpu.VMEM((chunks, np_ * nx, nz, rs, LANES), f32),
                pltpu.VMEM((chunks, wide, nz, rs, LANES), f32),
                pltpu.VMEM((chunks, nz, rs, LANES), f32),
                dma((chunks, wide)), dma((chunks, wide)),
                dma((chunks, wide)), dma((chunks, wide)),
                dma((chunks, nz)), dma((chunks, nz)),
                dma((chunks, nz)), dma((chunks, nz)),
                dma((chunks, nz, nx)), dma((chunks, nz, nx)),
            ],
            compiler_params=pltpu.CompilerParams(
                collective_id=0, has_side_effects=True, vmem_limit_bytes=60 * 1024 * 1024),
        )(activations, cotangents)

    in_specs = (P(("pair", "dp"), "ep"), P(("pair", "dp"), "ep"))
    return jax.shard_map(local, mesh=mesh, in_specs=in_specs, out_specs=P("pair", "ep"), check_vma=False)
```

time: 163 us -> 86.3 us (0.53)
  waiting for transfers between devices: 139 us -> 0 us
  Pallas kernels: 0 us -> 83.8 us
  between operations: 13.4 us -> 0.01 us
  matrix products: 4.9 us -> 0 us
  local copies, waits for them, and re-layouts: 4.19 us -> 2.3 us
    reduce_scatter x1 -> x0, waiting for transfers between devices: 100 us -> none  [local(): lax.psum_scatter(partial_grad, ('pair', 'dp'), scatter_dimension=0, tiled...]
    pallas_call x0 -> x1, Pallas kernels: none -> 83.8 us  [local(): pl.pallas_call(functools.partial(kernel, np_, nx, nz, nc, ns), out_shape=...]
    all_gather x1 -> x0, waiting for transfers between devices: 39.1 us -> none  [local(): return lax.all_gather(averaged, 'dp', axis=0, tiled=True)]
    dot_general x1 -> x0, matrix products: 4.9 us -> none  [local(): lax.dot_general(activations, cotangents, (((0,), (0,)), ((), ())), prefer...]
    unnamed x3 -> x1, local copies, waits for them, and re-layouts: 4.19 us -> 2.3 us
  transfers between devices with their start and end apart: 2 -> 0, of which waited for: 2 -> 0; matrix products, arithmetic and copies ran while one was open for 0% -> 0% of each run, Pallas kernels for 0% -> 0%
where the time goes in v1:
time: 86.3 us; the launch traced here: 86.1 us
  Pallas kernels  83.8 us (97%)
  local copies, waits for them, and re-layouts  2.3 us (3%)
    pallas_call x1, Pallas kernels, local(): pl.pallas_call(functools.partial(kernel, np_, nx, nz, nc, ns), out_shape=...  83.8 us
    unnamed x1, local copies, waits for them, and re-layouts  2.3 us

profile of v1, /device:TPU:0, one launch (start us, length us, event | category | flops | bytes accessed | tf_op | source)
XLA Modules:
  0.0 86.1 jit_solution(6461379457694144429)
XLA Ops:
  0.0 83.8 %shard_map.28 = bf16[256,2048]{1,0:T(8,128)(2,1)} custom-call(bf16[768,512]{1,0:T(8,128)(2,1)} %act_ref.1, bf16[768,2048]{1,0:T(8,128)(2,1)} %cot_ref.1), custom_call_target="tpu_custom_call" | custom-call | tf_op jit(solution)/shard_map/pallas_call | solution.py:242
  83.8 2.3 %copy.4 = bf16[256,2048]{1,0:T(8,128)(2,1)} copy(bf16[256,2048]{1,0:T(8,128)(2,1)} %shard_map.28) | data formatting | bytes 2097152

commit v2 on v1

--- a/solution.py
+++ b/solution.py
@@ -9,12 +9,13 @@
 
 LANES = 128
 SPLIT = 2
-AHEAD = 4
-CROSS = 4
-
-
-def kernel(np_, nx, nz, nc, ns, act_ref, cot_ref, out_ref, act_t, part, f1, f2, zr,
-           s1, r1, s2, r2, sz, rz, sg, rg, sx, rx):
+AHEAD = 3
+CROSS = 2
+LAG = (4, 7, 10)
+
+
+def kernel(np_, nx, nz, nc, ns, act_hbm, cot_hbm, out_ref, act_ref, cot_ref, act_t, part, f1, f2, zr,
+           s1, r1, s2, r2, sz, rz, sg, rg, sx, rx, load):
     p = lax.axis_index("pair")
     dp = lax.axis_index("dp")
     z, x = dp // nx, dp % nx
@@ -36,7 +37,7 @@
         return {"dp": other(z, q, nz) * nx + x}
 
     def crossed(k):
-        return lax.rem(k // ns, CROSS) == CROSS - 1
+        return lax.rem(k, CROSS) == CROSS - 1
 
     def remote(src, dst, ssem, rsem, peer):
         return pltpu.make_async_remote_copy(
@@ -181,41 +182,38 @@
     for peer in peers:
         pl.semaphore_signal(barrier, inc=1, device_id=peer, device_id_type=pl.DeviceIdType.MESH)
 
+    loads = [pltpu.make_async_copy(act_hbm, act_ref, load.at[0]), pltpu.make_async_copy(cot_hbm, cot_ref, load.at[1])]
+    for copy in loads:
+        copy.start()
+    loads[0].wait()
     act_t[...] = act_ref[...].T
-
-    def compute(c):
+    loads[1].wait()
+    width = 2 if nc % 2 == 0 else 1
+
+    @pl.loop(0, nc // width)
+    def _(g):
         for xi in range(nx):
-            col = pl.multiple_of(xi * cols_x + c * LANES, LANES)
-            grad = jnp.dot(act_t[...], cot_ref[:, pl.ds(col, LANES)], preferred_element_type=jnp.float32)
-            for pi in range(np_):
-                for zi in range(nz):
-                    for s in range(ns):
-                        row = pi * rows_p + (zi * ns + s) * rs
-                        part[c * ns + s, pi, xi, zi] = grad[row:row + rs]
-
-    compute(0)
+            col = pl.multiple_of(xi * cols_x + g * (width * LANES), LANES)
+            grad = jnp.dot(act_t[...], cot_ref[:, pl.ds(col, width * LANES)], preferred_element_type=jnp.float32)
+            for w in range(width):
+                for pi in range(np_):
+                    for zi in range(nz):
+                        for s in range(ns):
+                            row = pi * rows_p + (zi * ns + s) * rs
+                            part[(g * width + w) * ns + s, pi, xi, zi] = grad[row:row + rs, w * LANES:(w + 1) * LANES]
+
     pl.semaphore_wait(barrier, len(peers))
     ahead = min(AHEAD, chunks)
-
-    def send_ready(c):
-        for s in range(ns):
-            k = c * ns + s
-            pl.when(k < ahead)(functools.partial(start_first, k))
-
-    send_ready(0)
-
-    @pl.loop(1, nc)
-    def _(c):
-        compute(c)
-        send_ready(c)
-
-    @pl.loop(0, chunks + 3)
+    for k in range(ahead):
+        start_first(k)
+
+    @pl.loop(0, chunks + LAG[2])
     def _(t):
         pl.when(t + ahead < chunks)(lambda: start_first(t + ahead))
         pl.when(t < chunks)(lambda: stage2(t))
-        pl.when((t >= 1) & (t - 1 < chunks))(lambda: stage3(t - 1))
-        pl.when((t >= 2) & (t - 2 < chunks))(lambda: stage4(t - 2))
-        pl.when(t >= 3)(lambda: stage5(t - 3))
+        pl.when((t >= LAG[0]) & (t - LAG[0] < chunks))(lambda: stage3(t - LAG[0]))
+        pl.when((t >= LAG[1]) & (t - LAG[1] < chunks))(lambda: stage4(t - LAG[1]))
+        pl.when(t >= LAG[2])(lambda: stage5(t - LAG[2]))
 
     @pl.loop(0, chunks)
     def _(k):
@@ -242,9 +240,11 @@
         return pl.pallas_call(
             functools.partial(kernel, np_, nx, nz, nc, ns),
             out_shape=jax.ShapeDtypeStruct((rows // np_, cols), jnp.bfloat16),
-            in_specs=[pl.BlockSpec(memory_space=pltpu.VMEM)] * 2,
+            in_specs=[pl.BlockSpec(memory_space=pltpu.HBM)] * 2,
             out_specs=pl.BlockSpec(memory_space=pltpu.VMEM),
             scratch_shapes=[
+                pltpu.VMEM(activations.shape, activations.dtype),
+                pltpu.VMEM(cotangents.shape, cotangents.dtype),
                 pltpu.VMEM((rows, activations.shape[0]), activations.dtype),
                 pltpu.VMEM((chunks, np_, nx, nz, rs, LANES), f32),
                 pltpu.VMEM((chunks, np_ * nx, nz, rs, LANES), f32),
@@ -255,6 +255,7 @@
                 dma((chunks, nz)), dma((chunks, nz)),
                 dma((chunks, nz)), dma((chunks, nz)),
                 dma((chunks, nz, nx)), dma((chunks, nz, nx)),
+                dma((2,)),
             ],
             compiler_params=pltpu.CompilerParams(
                 collective_id=0, has_side_effects=True, vmem_limit_bytes=60 * 1024 * 1024),

time: 86.3 us -> 69.9 us (0.81)
  Pallas kernels: 83.8 us -> 67.4 us
    pallas_call x1, Pallas kernels: 83.8 us -> 67.4 us  [local(): pl.pallas_call(functools.partial(kernel, np_, nx, nz, nc, ns), out_shape=...]
where the time goes in v2:
time: 69.9 us; the launch traced here: 69.7 us
  Pallas kernels  67.4 us (96%)
  local copies, waits for them, and re-layouts  2.3 us (3%)
    pallas_call x1, Pallas kernels, local(): pl.pallas_call(functools.partial(kernel, np_, nx, nz, nc, ns), out_shape=...  67.4 us
    unnamed x1, local copies, waits for them, and re-layouts  2.3 us

profile of v2, /device:TPU:0, one launch (start us, length us, event | category | flops | bytes accessed | tf_op | source)
XLA Modules:
  0.0 69.7 jit_solution(14542833918828179150)
XLA Ops:
  0.0 67.4 %shard_map.28 = bf16[256,2048]{1,0:T(8,128)(2,1)} custom-call(bf16[768,512]{1,0:T(8,128)(2,1)} %act_hbm.1, bf16[768,2048]{1,0:T(8,128)(2,1)} %cot_hbm.1), custom_call_target="tpu_custom_call" | custom-call | tf_op jit(solution)/shard_map/pallas_call | solution.py:240
  67.4 2.3 %copy.4 = bf16[256,2048]{1,0:T(8,128)(2,1)} copy(bf16[256,2048]{1,0:T(8,128)(2,1)} %shard_map.28) | data formatting | bytes 2097152
